TPU v7x, 32 devices: a whole 2x2x4 slice. The times are simulated.
32 devices in a mesh: groups: 2 (over x), seq: 8 (over z, y), head: 2 (over core).
Axes of the slice: x: 2, y: 2, z: 4, core: 2. Of those that a mesh axis runs over, the one named last changes fastest.
Arguments:
- queries: bfloat16 [4096, 3584], P(('groups', 'seq'), 'head'), parts along dimension 0, may hold values from -30 to 30
- current_keys: bfloat16 [4096, 512], P(('groups', 'seq'), 'head'), parts along dimension 0, may hold values from -6 to 6
- current_values: bfloat16 [4096, 512], P(('groups', 'seq'), 'head'), parts along dimension 0, may hold values from -6 to 6
- stored_keys: bfloat16 [4096, 2, 512], P(('groups', 'seq'), None, 'head'), parts along dimension 0, may hold values from -22 to 22
- stored_values: bfloat16 [4096, 2, 512], P(('groups', 'seq'), None, 'head'), parts along dimension 0, may hold values from -6 to 6
- remap_table: int32 [3, 64], P(None, ('groups', 'seq')), parts along dimension 1, may hold values from 0 to 2047
- block_table: int32 [256], P('groups'), parts along dimension 0, may hold values from 0 to 15, as said below
Outputs:
- attended: bfloat16 [4096, 3584], P(('groups', 'seq'), 'head'), parts along dimension 0
- paged_keys: bfloat16 [4, 256, 2048], P('head', ('groups', 'seq')), parts along dimension 1
- paged_values: bfloat16 [4, 256, 2048], P('head', ('groups', 'seq')), parts along dimension 1
There are 2 independent parts, one for each index of `groups`. A program takes and returns all parts, laid end to end along the dimension named above; each array names one. Nothing has to cross between parts.
Inputs may be any that keep to these rules, and one draw needn't show every extreme that they name: `block_table`: the entries of the blocks b that share b modulo 8 are a permutation of 0 to 15.
All inputs are finite; a program needn't handle non-finite values.
Results may differ from a plain program's by a relative error of at most 0.012.
The roundings to bfloat16 on the way count: a program that leaves them out, or rounds other values in their place, can miss the bound.
Values may be sent and summed in bfloat16 or wider, within the bound.
A program may use at most 128 MiB of HBM per device.

v0:
```python
import math

import jax
import jax.numpy as jnp
from jax import lax
from jax.sharding import PartitionSpec as P

HEAD_SIZE = 128
PRIOR_SEGMENTS = 2
PAGE_TOKENS = 16
QBLK = 64


rope_base = 1000000.0
masked_value = -1e30


def apply_rotary(values, token_positions):
    half_dim = values.shape[-1] // 2
    frequency = rope_base ** (-2.0 * jnp.arange(half_dim, dtype=jnp.float32) / values.shape[-1])
    angles = token_positions.astype(jnp.float32)[:, None] * frequency[None, :]
    cos_table = jnp.cos(angles)[:, None, :]
    sin_table = jnp.sin(angles)[:, None, :]
    first_half = values[..., :half_dim]
    second_half = values[..., half_dim:]
    return jnp.concatenate(
        [
            first_half * cos_table - second_half * sin_table,
            second_half * cos_table + first_half * sin_table,
        ],
        -1,
    )


def update_block(state, query_rows, key_tile, value_tile, allowed):
    running_max, denom, accumulated = state
    scores = jnp.einsum(
        "grd,gkd->grk", query_rows, key_tile, preferred_element_type=jnp.float32
    ) * query_rows.shape[-1] ** (-0.5)
    if allowed is not None:
        scores = jnp.where(allowed[None], scores, masked_value)
    new_max = jnp.maximum(running_max, jnp.max(scores, -1))
    factor = jnp.exp(running_max - new_max)
    weights = jnp.exp(scores - new_max[..., None])
    if allowed is not None:
        weights = jnp.where(allowed[None], weights, 0.0)
    denom = denom * factor + jnp.sum(weights, -1)
    product = jnp.einsum(
        "grk,gkd->grd", weights.astype(jnp.bfloat16), value_tile, preferred_element_type=jnp.float32
    )
    accumulated = accumulated * factor[..., None] + product
    return (new_max, denom, accumulated)


def attend(state, query_rows, keys, values, row_token, last_token, causal):
    kv_local = query_rows.shape[0]
    head_dim = query_rows.shape[-1]
    key_count = keys.shape[0]
    key_block = math.gcd(key_count, 256)

    def step_body(step_index, held_state):
        offset = step_index * key_block
        key_tile = (
            lax.dynamic_slice_in_dim(keys, offset, key_block, 0)
            .reshape(key_block, kv_local, head_dim)
            .transpose(1, 0, 2)
        )
        value_tile = (
            lax.dynamic_slice_in_dim(values, offset, key_block, 0)
            .reshape(key_block, kv_local, head_dim)
            .transpose(1, 0, 2)
        )
        if causal:
            key_index = offset + jnp.arange(key_block, dtype=jnp.int32)
            allowed = key_index[None, :] <= row_token[:, None]
            return lax.cond(
                offset <= last_token,
                lambda inner: update_block(inner, query_rows, key_tile, value_tile, allowed),
                lambda inner: inner,
                held_state,
            )
        return update_block(held_state, query_rows, key_tile, value_tile, None)

    return lax.fori_loop(0, key_count // key_block, step_body, state)


def shards(
    queries, current_keys, current_values, stored_keys, stored_values, remap_table, block_table
):
    tok_rows = queries.shape[0]
    kv_local = current_keys.shape[1] // HEAD_SIZE
    per_group = queries.shape[1] // (kv_local * HEAD_SIZE)
    my_index = lax.axis_index("seq")
    owners = lax.axis_size("seq")
    token_positions = (
        jnp.repeat(remap_table, QBLK, axis=1)
        + (jnp.arange(tok_rows, dtype=jnp.int32) % QBLK)[None, :]
    )
    query_single_float = queries.astype(jnp.float32).reshape(
        tok_rows, kv_local * per_group, HEAD_SIZE
    )
    rotary_output = []
    for segment_kind_index in range(3):
        turned = apply_rotary(query_single_float, token_positions[segment_kind_index]).astype(
            jnp.bfloat16
        )
        rotary_output.append(
            turned.reshape(tok_rows, kv_local, per_group, HEAD_SIZE)
            .transpose(1, 0, 2, 3)
            .reshape(kv_local, tok_rows * per_group, HEAD_SIZE)
        )
    row_count = tok_rows * per_group
    row_token = my_index * tok_rows + jnp.arange(row_count, dtype=jnp.int32) // per_group
    last_token = my_index * tok_rows + tok_rows - 1
    state = (
        jnp.full((kv_local, row_count), masked_value, jnp.float32),
        jnp.zeros((kv_local, row_count), jnp.float32),
        jnp.zeros((kv_local, row_count, HEAD_SIZE), jnp.float32),
    )
    pages_here = tok_rows // PAGE_TOKENS
    paged = jnp.zeros((2, kv_local, pages_here, PAGE_TOKENS * HEAD_SIZE), jnp.bfloat16)
    pieces = (
        lax.all_gather(stored_keys, "seq", axis=0, tiled=True),
        lax.all_gather(stored_values, "seq", axis=0, tiled=True),
    )
    held_state = state
    piece_keys = pieces[0]
    piece_values = pieces[1]
    for segment_number in range(PRIOR_SEGMENTS):
        query_rows = rotary_output[2] if segment_number < PRIOR_SEGMENTS - 1 else rotary_output[1]
        held_state = attend(
            held_state,
            query_rows,
            piece_keys[:, segment_number, :],
            piece_values[:, segment_number, :],
            row_token,
            last_token,
            False,
        )
    state, paged = (held_state, paged)
    pieces = (
        lax.all_gather(current_keys, "seq", axis=0, tiled=True),
        lax.all_gather(current_values, "seq", axis=0, tiled=True),
    )
    state = attend(state, rotary_output[0], pieces[0], pieces[1], row_token, last_token, True)
    rounds = pages_here // owners
    previous = jnp.stack(
        [stored_keys[:, PRIOR_SEGMENTS - 1, :], stored_values[:, PRIOR_SEGMENTS - 1, :]]
    )
    arranged = (
        previous.reshape(2, rounds, owners, PAGE_TOKENS, kv_local, HEAD_SIZE)
        .transpose(0, 4, 1, 2, 3, 5)
        .reshape(2, kv_local, rounds, owners, PAGE_TOKENS * HEAD_SIZE)
    )
    received = lax.all_to_all(arranged, "seq", split_axis=3, concat_axis=3, tiled=True)
    source_index = jnp.arange(owners, dtype=jnp.int32)[None, :]
    round_index = jnp.arange(rounds, dtype=jnp.int32)[:, None]
    block_index = source_index * pages_here + round_index * owners + my_index
    target = block_table[block_index.reshape(-1)]
    paged = paged.at[:, :, target].set(
        received.reshape(2, kv_local, rounds * owners, PAGE_TOKENS * HEAD_SIZE)
    )
    finished = state[2] / state[1][..., None]
    attended = (
        finished.reshape(kv_local, tok_rows, per_group, HEAD_SIZE)
        .transpose(1, 0, 2, 3)
        .reshape(tok_rows, kv_local * per_group * HEAD_SIZE)
        .astype(jnp.bfloat16)
    )
    return (attended, paged[0], paged[1])


def solution(mesh):
    in_specs = (
        P(("groups", "seq"), "head"),
        P(("groups", "seq"), "head"),
        P(("groups", "seq"), "head"),
        P(("groups", "seq"), None, "head"),
        P(("groups", "seq"), None, "head"),
        P(None, ("groups", "seq")),
        P("groups"),
    )
    out_specs = (
        P(("groups", "seq"), "head"),
        P("head", ("groups", "seq"), None),
        P("head", ("groups", "seq"), None),
    )
    return jax.shard_map(shards, mesh=mesh, in_specs=in_specs, out_specs=out_specs, check_vma=False)
```

profile of v0, /device:TPU:28, one launch (start us, length us, event | category | flops | bytes accessed | tf_op | source)
XLA Modules:
  0.0 327.9 jit_solution(3574212434276726992)
XLA Ops:
  15.7 6.0 %all-to-all-start = ((bf16[2,2,2,8,2048]{4,2,1,0,3:T(2,128)(2,1)}), bf16[2,2,2,8,2048]{4,2,1,0,3:T(2,128)(2,1)S(1)}, u32[]{:S(2)}, u32[]{:S(2)}) async-start(bf16[2,2,2,8,2048]{4,2,1,0,3:T(2,128)(2,1)} %reshape.367), calls=%async_computation | async-start | bytes 524288 | tf_op jit(solution)/shard_map/all_to_all | solution.py:155
  31.9 3.6 %copy.83 = bf16[2,256,7,128]{3,0,2,1:T(2,128)(2,1)} copy(bf16[2,256,7,128]{1,3,2,0:T(8,128)(2,1)} %maximum_bitcast_fusion) | data formatting | bytes 1835008 | tf_op jit(solution)/shard_map/transpose | solution.py:109
  38.9 3.6 %copy.90 = bf16[2,256,7,128]{3,0,2,1:T(2,128)(2,1)} copy(bf16[2,256,7,128]{1,3,2,0:T(8,128)(2,1)} %maximum_bitcast_fusion.2) | data formatting | bytes 1835008 | tf_op jit(solution)/shard_map/transpose | solution.py:109
  49.0 14.1 %all-gather.5.cloned.1.call-done = bf16[2048,2,256]{0,2,1:T(8,128)(2,1)} async-done(((bf16[256,2,256]{0,2,1:T(8,128)(2,1)}), bf16[2048,2,256]{0,2,1:T(8,128)(2,1)}) %all-gather.5.cloned.1.call-update) | async-done | bytes 2097168 | tf_op jit(solution)/shard_map/all_gather | solution.py:123
  66.3 47.4 %all-gather.7.cloned.1.call-done = bf16[2048,2,256]{0,2,1:T(8,128)(2,1)} async-done(((bf16[256,2,256]{0,2,1:T(8,128)(2,1)}), bf16[2048,2,256]{0,2,1:T(8,128)(2,1)}) %all-gather.7.cloned.1.call-update) | async-done | bytes 2097168 | tf_op jit(solution)/shard_map/all_gather | solution.py:124
  116.8 85.0 %while.55 = (s32[]{:T(128)}, f32[2,1792]{1,0:T(2,128)S(1)}, f32[2,1792]{1,0:T(2,128)S(1)}, f32[2,1792,128]{2,1,0:T(8,128)S(1)}, bf16[2048,256]{0,1:T(8,128)(2,1)...) while((s32[]{:T(128)}, f32[2,1792]{1,0:T(2,128)S(1)}, ...), condition=%wide.region_3.4_spmd.clone, body=%wide.region_0.3_spmd.clone.sunk | while | flops 478496256 | bytes 17137836 | solution.py:84
  118.0 3.6 %bitcast_reduce_fusion.5 = (f32[2,1792]{1,0:T(2,128)S(1)}, f32[2,256,1792]{2,1,0:T(8,128)}) fusion(bf16[2,1792,128]{2,1,0:T(8,128)(2,1)} %get-tuple-element.975, bf16[256,2,128]{2,0,1:T(8,128)(2,1)S(1)} %copy.116), kind=kOutput, calls=%fused_computation.20.clone.1 | convolution fusion | flops 236712448 | bytes 4732928 | tf_op jit(solution)/shard_map/while/body/eval_jaxpr/grd,gkd->grk/dot_general | solution.py:37
  128.6 3.6 %bitcast_reduce_fusion.5 = (f32[2,1792]{1,0:T(2,128)S(1)}, f32[2,256,1792]{2,1,0:T(8,128)}) fusion(bf16[2,1792,128]{2,1,0:T(8,128)(2,1)} %get-tuple-element.975, bf16[256,2,128]{2,0,1:T(8,128)(2,1)S(1)} %copy.116), kind=kOutput, calls=%fused_computation.20.clone.1 | convolution fusion | flops 236712448 | bytes 4732928 | tf_op jit(solution)/shard_map/while/body/eval_jaxpr/grd,gkd->grk/dot_general | solution.py:37
  139.2 3.6 %bitcast_reduce_fusion.5 = (f32[2,1792]{1,0:T(2,128)S(1)}, f32[2,256,1792]{2,1,0:T(8,128)}) fusion(bf16[2,1792,128]{2,1,0:T(8,128)(2,1)} %get-tuple-element.975, bf16[256,2,128]{2,0,1:T(8,128)(2,1)S(1)} %copy.116), kind=kOutput, calls=%fused_computation.20.clone.1 | convolution fusion | flops 236712448 | bytes 4732928 | tf_op jit(solution)/shard_map/while/body/eval_jaxpr/grd,gkd->grk/dot_general | solution.py:37
  149.8 3.6 %bitcast_reduce_fusion.5 = (f32[2,1792]{1,0:T(2,128)S(1)}, f32[2,256,1792]{2,1,0:T(8,128)}) fusion(bf16[2,1792,128]{2,1,0:T(8,128)(2,1)} %get-tuple-element.975, bf16[256,2,128]{2,0,1:T(8,128)(2,1)S(1)} %copy.116), kind=kOutput, calls=%fused_computation.20.clone.1 | convolution fusion | flops 236712448 | bytes 4732928 | tf_op jit(solution)/shard_map/while/body/eval_jaxpr/grd,gkd->grk/dot_general | solution.py:37
  160.4 3.6 %bitcast_reduce_fusion.5 = (f32[2,1792]{1,0:T(2,128)S(1)}, f32[2,256,1792]{2,1,0:T(8,128)}) fusion(bf16[2,1792,128]{2,1,0:T(8,128)(2,1)} %get-tuple-element.975, bf16[256,2,128]{2,0,1:T(8,128)(2,1)S(1)} %copy.116), kind=kOutput, calls=%fused_computation.20.clone.1 | convolution fusion | flops 236712448 | bytes 4732928 | tf_op jit(solution)/shard_map/while/body/eval_jaxpr/grd,gkd->grk/dot_general | solution.py:37
  181.7 3.7 %bitcast_reduce_fusion.5 = (f32[2,1792]{1,0:T(2,128)S(1)}, f32[2,256,1792]{2,1,0:T(8,128)}) fusion(bf16[2,1792,128]{2,1,0:T(8,128)(2,1)} %get-tuple-element.975, bf16[256,2,128]{2,0,1:T(8,128)(2,1)S(1)} %copy.116), kind=kOutput, calls=%fused_computation.20.clone.1 | convolution fusion | flops 236712448 | bytes 4732928 | tf_op jit(solution)/shard_map/while/body/eval_jaxpr/grd,gkd->grk/dot_general | solution.py:37
  192.4 3.6 %bitcast_reduce_fusion.5 = (f32[2,1792]{1,0:T(2,128)S(1)}, f32[2,256,1792]{2,1,0:T(8,128)}) fusion(bf16[2,1792,128]{2,1,0:T(8,128)(2,1)} %get-tuple-element.975, bf16[256,2,128]{2,0,1:T(8,128)(2,1)S(1)} %copy.116), kind=kOutput, calls=%fused_computation.20.clone.1 | convolution fusion | flops 236712448 | bytes 4732928 | tf_op jit(solution)/shard_map/while/body/eval_jaxpr/grd,gkd->grk/dot_general | solution.py:37
  201.9 59.0 %while.53 = (s32[]{:T(128)}, f32[2,1792]{1,0:T(2,128)S(1)}, f32[2,1792]{1,0:T(2,128)S(1)}, f32[2,1792,128]{2,1,0:T(8,128)S(1)}, bf16[2048,256]{0,1:T(8,128)(2,1)...) while((s32[]{:T(128)}, f32[2,1792]{1,0:T(2,128)S(1)}, ...), condition=%wide.region_7.8_spmd, body=%wide.region_4.7_spmd.sunk | while | flops 478026752 | bytes 31817916 | solution.py:84
  260.9 49.5 %while.54 = (s32[]{:T(128)}, f32[2,1792]{1,0:T(2,128)S(1)}, f32[2,1792]{1,0:T(2,128)S(1)}, f32[2,1792,128]{2,1,0:T(8,128)S(1)}, s32[]{:T(128)}, /*index=5*/bf16[...) while((s32[]{:T(128)}, f32[2,1792]{1,0:T(2,128)S(1)}, ...), condition=%wide.region_13.14_spmd.clone, body=%wide.region_8.13_spmd.clone.sunk | while | flops 479419392 | bytes 18524560 | solution.py:84
  262.2 5.1 %conditional.3 = ((f32[2,1792]{1,0:T(2,128)S(1)}, f32[2,1792]{1,0:T(2,128)S(1)}, f32[2,1792,128]{2,1,0:T(8,128)S(1)})) conditional(s32[]{:T(128)} %convert_element_type.100, (f32[2,1792]{1,0:T(2,128)S(1)}, f32[2,1792]{1,0:T(2,128)S(1)}, f32[2,1792,128]{2,1,0:T(8,128)S(1)}) %tuple.153, (s32[]{:T(128)}, s32[1,256]{1,0:T(1,128)S(1)}, s32[]{:T(128)}, ...), branch_computations={%region_9.9_spmd, %region_10.12_spmd.clone} | conditional | flops 479417600 | bytes 17977392 | solution.py:76
  268.4 5.1 %conditional.3 = ((f32[2,1792]{1,0:T(2,128)S(1)}, f32[2,1792]{1,0:T(2,128)S(1)}, f32[2,1792,128]{2,1,0:T(8,128)S(1)})) conditional(s32[]{:T(128)} %convert_element_type.100, (f32[2,1792]{1,0:T(2,128)S(1)}, f32[2,1792]{1,0:T(2,128)S(1)}, f32[2,1792,128]{2,1,0:T(8,128)S(1)}) %tuple.153, (s32[]{:T(128)}, s32[1,256]{1,0:T(1,128)S(1)}, s32[]{:T(128)}, ...), branch_computations={%region_9.9_spmd, %region_10.12_spmd.clone} | conditional | flops 479417600 | bytes 17977392 | solution.py:76
  274.6 5.1 %conditional.3 = ((f32[2,1792]{1,0:T(2,128)S(1)}, f32[2,1792]{1,0:T(2,128)S(1)}, f32[2,1792,128]{2,1,0:T(8,128)S(1)})) conditional(s32[]{:T(128)} %convert_element_type.100, (f32[2,1792]{1,0:T(2,128)S(1)}, f32[2,1792]{1,0:T(2,128)S(1)}, f32[2,1792,128]{2,1,0:T(8,128)S(1)}) %tuple.153, (s32[]{:T(128)}, s32[1,256]{1,0:T(1,128)S(1)}, s32[]{:T(128)}, ...), branch_computations={%region_9.9_spmd, %region_10.12_spmd.clone} | conditional | flops 479417600 | bytes 17977392 | solution.py:76
  280.7 5.1 %conditional.3 = ((f32[2,1792]{1,0:T(2,128)S(1)}, f32[2,1792]{1,0:T(2,128)S(1)}, f32[2,1792,128]{2,1,0:T(8,128)S(1)})) conditional(s32[]{:T(128)} %convert_element_type.100, (f32[2,1792]{1,0:T(2,128)S(1)}, f32[2,1792]{1,0:T(2,128)S(1)}, f32[2,1792,128]{2,1,0:T(8,128)S(1)}) %tuple.153, (s32[]{:T(128)}, s32[1,256]{1,0:T(1,128)S(1)}, s32[]{:T(128)}, ...), branch_computations={%region_9.9_spmd, %region_10.12_spmd.clone} | conditional | flops 479417600 | bytes 17977392 | solution.py:76
  286.9 5.1 %conditional.3 = ((f32[2,1792]{1,0:T(2,128)S(1)}, f32[2,1792]{1,0:T(2,128)S(1)}, f32[2,1792,128]{2,1,0:T(8,128)S(1)})) conditional(s32[]{:T(128)} %convert_element_type.100, (f32[2,1792]{1,0:T(2,128)S(1)}, f32[2,1792]{1,0:T(2,128)S(1)}, f32[2,1792,128]{2,1,0:T(8,128)S(1)}) %tuple.153, (s32[]{:T(128)}, s32[1,256]{1,0:T(1,128)S(1)}, s32[]{:T(128)}, ...), branch_computations={%region_9.9_spmd, %region_10.12_spmd.clone} | conditional | flops 479417600 | bytes 17977392 | solution.py:76
  293.0 5.1 %conditional.3 = ((f32[2,1792]{1,0:T(2,128)S(1)}, f32[2,1792]{1,0:T(2,128)S(1)}, f32[2,1792,128]{2,1,0:T(8,128)S(1)})) conditional(s32[]{:T(128)} %convert_element_type.100, (f32[2,1792]{1,0:T(2,128)S(1)}, f32[2,1792]{1,0:T(2,128)S(1)}, f32[2,1792,128]{2,1,0:T(8,128)S(1)}) %tuple.153, (s32[]{:T(128)}, s32[1,256]{1,0:T(1,128)S(1)}, s32[]{:T(128)}, ...), branch_computations={%region_9.9_spmd, %region_10.12_spmd.clone} | conditional | flops 479417600 | bytes 17977392 | solution.py:76
  299.2 5.1 %conditional.3 = ((f32[2,1792]{1,0:T(2,128)S(1)}, f32[2,1792]{1,0:T(2,128)S(1)}, f32[2,1792,128]{2,1,0:T(8,128)S(1)})) conditional(s32[]{:T(128)} %convert_element_type.100, (f32[2,1792]{1,0:T(2,128)S(1)}, f32[2,1792]{1,0:T(2,128)S(1)}, f32[2,1792,128]{2,1,0:T(8,128)S(1)}) %tuple.153, (s32[]{:T(128)}, s32[1,256]{1,0:T(1,128)S(1)}, s32[]{:T(128)}, ...), branch_computations={%region_9.9_spmd, %region_10.12_spmd.clone} | conditional | flops 479417600 | bytes 17977392 | solution.py:76
  305.3 5.1 %conditional.3 = ((f32[2,1792]{1,0:T(2,128)S(1)}, f32[2,1792]{1,0:T(2,128)S(1)}, f32[2,1792,128]{2,1,0:T(8,128)S(1)})) conditional(s32[]{:T(128)} %convert_element_type.100, (f32[2,1792]{1,0:T(2,128)S(1)}, f32[2,1792]{1,0:T(2,128)S(1)}, f32[2,1792,128]{2,1,0:T(8,128)S(1)}) %tuple.153, (s32[]{:T(128)}, s32[1,256]{1,0:T(1,128)S(1)}, s32[]{:T(128)}, ...), branch_computations={%region_9.9_spmd, %region_10.12_spmd.clone} | conditional | flops 479417600 | bytes 17977392 | solution.py:76
  311.0 7.6 %copy.92 = bf16[2,1792,128]{2,0,1:T(2,128)(2,1)S(1)} copy(bf16[2,1792,128]{2,1,0:T(8,128)(2,1)S(1)} %divide_convert_fusion) | data formatting | bytes 1835008 | tf_op jit(solution)/shard_map/convert_element_type | solution.py:168
  (345 shorter events, 203.9 us)
Async XLA Ops:
  7.2 37.8 %copy-start = (s32[128]{0:T(128)S(1)}, s32[128]{0:T(128)}, u32[]{:S(2)}) copy-start(s32[128]{0:T(128)} %param.21) | copy-start | bytes 1540
  7.2 5.6 %copy-start.6 = (bf16[256,2,256]{2,1,0:T(2,128)(2,1)S(1)}, bf16[256,2,256]{2,1,0:T(2,128)(2,1)}, u32[]{:S(2)}) copy-start(bf16[256,2,256]{2,1,0:T(2,128)(2,1)} %param.18) | copy-start | bytes 786436
  7.2 6.4 %copy-start.7 = (bf16[256,2,256]{2,1,0:T(2,128)(2,1)S(1)}, bf16[256,2,256]{2,1,0:T(2,128)(2,1)}, u32[]{:S(2)}) copy-start(bf16[256,2,256]{2,1,0:T(2,128)(2,1)} %param.19) | copy-start | bytes 786436
  7.2 55.9 %all-gather.5.cloned.1.call-start = ((), (), s32[]{:S(2)}) async-start(), calls=%async_computation.1 | async-start | bytes 2359296 | tf_op jit(solution)/shard_map/all_gather | solution.py:123
  9.1 104.6 %all-gather.7.cloned.1.call-start = ((), (), s32[]{:S(2)}) async-start(), calls=%async_computation.2 | async-start | bytes 2359296 | tf_op jit(solution)/shard_map/all_gather | solution.py:124
  11.0 10.6 %copy-start.8 = (bf16[256,256]{1,0:T(8,128)(2,1)S(1)}, bf16[256,256]{1,0:T(8,128)(2,1)}, u32[]{:S(2)}) copy-start(bf16[256,256]{1,0:T(8,128)(2,1)} %param.16) | copy-start | bytes 393220
  11.0 11.5 %copy-start.9 = (s32[3,4]{1,0:T(4,128)S(1)}, s32[3,4]{1,0:T(4,128)}, u32[]{:S(2)}) copy-start(s32[3,4]{1,0:T(4,128)} %param.20) | copy-start | bytes 148
  11.1 249.9 %all-gather.11.cloned.1.call-start = ((), (), s32[]{:S(2)}) async-start(), calls=%async_computation.4 | async-start | bytes 1179648 | tf_op jit(solution)/shard_map/all_gather | solution.py:143
  15.7 30.0 %all-to-all-start = ((bf16[2,2,2,8,2048]{4,2,1,0,3:T(2,128)(2,1)}), bf16[2,2,2,8,2048]{4,2,1,0,3:T(2,128)(2,1)S(1)}, u32[]{:S(2)}, u32[]{:S(2)}) async-start(bf16[2,2,2,8,2048]{4,2,1,0,3:T(2,128)(2,1)} %reshape.367), calls=%async_computation | async-start | bytes 524288 | tf_op jit(solution)/shard_map/all_to_all | solution.py:155
  21.7 239.3 %all-gather.9.cloned.1.call-start = ((), (), s32[]{:S(2)}) async-start(), calls=%async_computation.3 | async-start | bytes 1179648 | tf_op jit(solution)/shard_map/all_gather | solution.py:142
  29.4 1.4 copy-start.4
  29.4 1.4 copy-start.5
  35.5 2.3 copy-start.2
  35.5 2.3 copy-start.3
  203.7 1.8 copy-start.1
  211.0 1.8 copy-start.1
  218.4 1.8 copy-start.1
  225.8 1.8 copy-start.1
  233.2 1.8 copy-start.1
  240.6 1.8 copy-start.1
  247.9 1.8 copy-start.1
  255.3 1.8 copy-start.1
Sparse Core Ops, SparseCore 0:
  10.1 52.9 all-gather.4
  65.1 48.5 all-gather.6
  115.7 38.2 all-gather.10
  155.9 38.3 all-gather.8
where the time goes:
time: 330 us; the launch traced here: 328 us
  matrix products  112 us (34%)
  local copies, waits for them, and re-layouts  88.5 us (27%)
  waiting for transfers between devices  61.6 us (19%)
  other arithmetic  43.5 us (13%)
  between operations  14.1 us (4%)
  starting transfers between devices  6.12 us (2%)
    dot_general x24, matrix products, update_block(): jnp.einsum('grk,gkd->grd', weights.astype(jnp.bfloat16), value_tile, pref...  60.7 us
    dot_general x24, matrix products, update_block(): jnp.einsum('grd,gkd->grk', query_rows, key_tile, preferred_element_type=j...  51.2 us
    all_gather x1, waiting for transfers between devices, shards(): lax.all_gather(stored_values, 'seq', axis=0, tiled=True)  47.4 us
    reduce_sum x24, other arithmetic, update_block(): denom = denom * factor + jnp.sum(weights, -1)  32.5 us
    dynamic_slice x24, local copies, waits for them, and re-layouts, step_body(): lax.dynamic_slice_in_dim(values, offset, key_block, 0)  23.8 us
    unnamed x28, local copies, waits for them, and re-layouts  14.9 us
    while x32, local copies, waits for them, and re-layouts  14.1 us
    all_gather x1, waiting for transfers between devices, shards(): lax.all_gather(stored_keys, 'seq', axis=0, tiled=True)  14.1 us
  transfers between devices with their start and end apart: 5, of which 2 were waited for; matrix products, arithmetic and copies ran while one was open for 51% of the time, Pallas kernels for 0%

commit v1 on v0

v1 whole, which is shorter than its diff:
```python
import functools
import math

import jax
import jax.numpy as jnp
from jax import lax
from jax.experimental import pallas as pl
from jax.experimental.pallas import tpu as pltpu
from jax.sharding import PartitionSpec as P

HEAD_SIZE = 128
PRIOR_SEGMENTS = 2
PAGE_TOKENS = 16
QBLK = 64
KINDS = PRIOR_SEGMENTS + 1
OWN_PART = PRIOR_SEGMENTS

rope_base = 1000000.0
masked_value = -1e30
MESH = pl.DeviceIdType.MESH
RIGHT, LEFT, ACROSS = 0, 1, 2


def kernel(
    n, kv_local, per_group, q_ref, cos_ref, sin_ref, kv_hbm, out_ref, raw_ref,
    held, turned, top, denom, total, own_sem, send_sem, recv_sem,
):
    me = lax.axis_index("seq")
    partner = me + 1 - 2 * (me % 2)
    tokens = q_ref.shape[0]
    heads = kv_local * per_group
    scale = HEAD_SIZE ** -0.5 * math.log2(math.e)
    has_right = me + 2 < n
    has_left = me - 2 >= 0

    own = pltpu.make_async_copy(kv_hbm, held.at[me], own_sem)
    own.start()
    barrier = pltpu.get_barrier_semaphore()
    pl.semaphore_signal(barrier, inc=1, device_id={"seq": partner}, device_id_type=MESH)

    @pl.when(has_right)
    def _():
        pl.semaphore_signal(barrier, inc=1, device_id={"seq": me + 2}, device_id_type=MESH)

    @pl.when(has_left)
    def _():
        pl.semaphore_signal(barrier, inc=1, device_id={"seq": me - 2}, device_id_type=MESH)

    expected = 1 + has_right.astype(jnp.int32) + has_left.astype(jnp.int32)
    pl.semaphore_wait(barrier, expected)
    own.wait()

    def remote(way, j, part):
        target = (me + 2, me - 2, partner)[way]
        return pltpu.make_async_remote_copy(
            src_ref=held.at[j, part],
            dst_ref=held.at[j, part],
            send_sem=send_sem.at[way, j, part],
            recv_sem=recv_sem.at[j, part],
            device_id={"seq": target},
            device_id_type=MESH,
        )

    def goes(way, j, part):
        mine = (j % 2) == (me % 2)
        stored = part < PRIOR_SEGMENTS
        if way == RIGHT:
            return mine & (j <= me) & has_right
        if way == LEFT:
            return mine & (j >= me) & stored & has_left
        return mine & (stored | (j <= partner))

    def forward(j, part):
        for way in (ACROSS, RIGHT, LEFT):

            @pl.when(goes(way, j, part))
            def _():
                remote(way, j, part).start()

    for part in range(KINDS):
        forward(me, part)

    def turn(part, carry):
        cos = cos_ref[part]
        sin = sin_ref[part]
        for h in range(heads):
            x = q_ref[:, h * HEAD_SIZE : (h + 1) * HEAD_SIZE].astype(jnp.float32)
            y = x * cos + pltpu.roll(x, HEAD_SIZE // 2, 1) * sin
            turned[part, h] = y.astype(jnp.bfloat16)
        return carry

    lax.fori_loop(0, KINDS, turn, 0)
    top[...] = jnp.full(top.shape, masked_value, jnp.float32)
    denom[...] = jnp.zeros(denom.shape, jnp.float32)
    total[...] = jnp.zeros(total.shape, jnp.float32)

    def absorb(j, part, causal):
        for g in range(kv_local):
            columns = slice(g * HEAD_SIZE, (g + 1) * HEAD_SIZE)
            keys = held[j, part, 0, :, columns]
            values = held[j, part, 1, :, columns].T
            for r in range(per_group):
                h = g * per_group + r
                scores = lax.dot_general(
                    keys, turned[part, h], (((1,), (1,)), ((), ())),
                    preferred_element_type=jnp.float32,
                )
                if causal:
                    key_index = lax.broadcasted_iota(jnp.int32, scores.shape, 0)
                    row_index = lax.broadcasted_iota(jnp.int32, scores.shape, 1)
                    scores = jnp.where(key_index <= row_index, scores, masked_value)
                old = top[h]
                new = jnp.maximum(old, jnp.max(scores, 0, keepdims=True))
                factor = jnp.exp2((old - new) * scale)
                weights = jnp.exp2((scores - new) * scale)
                top[h] = new
                denom[h] = denom[h] * factor + jnp.sum(weights, 0, keepdims=True)
                total[h] = total[h] * factor + jnp.dot(
                    values, weights.astype(jnp.bfloat16), preferred_element_type=jnp.float32
                )

    def own_step(part, carry):
        absorb(me, part, False)
        return carry

    lax.fori_loop(0, PRIOR_SEGMENTS, own_step, 0)
    absorb(me, OWN_PART, True)

    def round_step(step, carry):
        distance = step // (4 * KINDS) + 1
        part = (step // 4) % KINDS
        kind = step % 4
        near = distance - kind // 2
        start = jnp.where(kind < 2, me, partner)
        sign = 1 - 2 * (kind % 2)
        j = start - sign * 2 * near
        stored = part < PRIOR_SEGMENTS
        wanted = (j >= 0) & (j < n) & (stored | (j <= me)) & ((near > 0) | (kind % 2 == 0))

        @pl.when(wanted)
        def _():
            remote(RIGHT, j, part).wait_recv()
            forward(j, part)
            absorb(j, part, False)

        return carry

    lax.fori_loop(0, (n // 2) * 4 * KINDS, round_step, 0)

    rounds = tokens // PAGE_TOKENS // n
    last = PRIOR_SEGMENTS - 1

    def page_step(j, carry):
        for r in range(rounds):
            rows = pl.ds(pl.multiple_of((r * n + me) * PAGE_TOKENS, PAGE_TOKENS), PAGE_TOKENS)
            for which in range(2):
                raw_ref[which, j * rounds + r] = held[j, last, which, rows, :]
        return carry

    lax.fori_loop(0, n, page_step, 0)

    for h in range(heads):
        finished = total[h] / denom[h]
        out_ref[:, h * HEAD_SIZE : (h + 1) * HEAD_SIZE] = finished.T.astype(out_ref.dtype)

    def drain(step, carry):
        j = step // KINDS
        part = step % KINDS
        for way in (ACROSS, RIGHT, LEFT):

            @pl.when(goes(way, j, part))
            def _():
                remote(way, j, part).wait_send()

        return carry

    lax.fori_loop(0, n * KINDS, drain, 0)


def shards(
    queries, current_keys, current_values, stored_keys, stored_values, remap_table, block_table
):
    tokens, width = queries.shape
    key_width = current_keys.shape[1]
    kv_local = key_width // HEAD_SIZE
    heads = width // HEAD_SIZE
    per_group = heads // kv_local
    my_index = lax.axis_index("seq")
    owners = lax.axis_size("seq")
    positions = (
        jnp.repeat(remap_table, QBLK, axis=1)
        + (jnp.arange(tokens, dtype=jnp.int32) % QBLK)[None, :]
    )
    positions = jnp.stack([positions[2], positions[1], positions[0]])
    half_dim = HEAD_SIZE // 2
    frequency = rope_base ** (-2.0 * jnp.arange(half_dim, dtype=jnp.float32) / HEAD_SIZE)
    angles = positions.astype(jnp.float32)[..., None] * frequency
    cos = jnp.cos(angles)
    sin = jnp.sin(angles)
    cos = jnp.concatenate([cos, cos], -1)
    sin = jnp.concatenate([-sin, sin], -1)
    kv = jnp.stack(
        [
            jnp.stack([stored_keys[:, s, :], stored_values[:, s, :]])
            for s in range(PRIOR_SEGMENTS)
        ]
        + [jnp.stack([current_keys, current_values])]
    )
    rounds = tokens // PAGE_TOKENS // owners
    vmem = pl.BlockSpec(memory_space=pltpu.VMEM)
    attended, raw = pl.pallas_call(
        functools.partial(kernel, owners, kv_local, per_group),
        out_shape=(
            jax.ShapeDtypeStruct((tokens, width), jnp.bfloat16),
            jax.ShapeDtypeStruct((2, owners * rounds, PAGE_TOKENS, key_width), jnp.bfloat16),
        ),
        in_specs=[vmem, vmem, vmem, pl.BlockSpec(memory_space=pl.ANY)],
        out_specs=(vmem, vmem),
        scratch_shapes=[
            pltpu.VMEM((owners, KINDS, 2, tokens, key_width), jnp.bfloat16),
            pltpu.VMEM((KINDS, heads, tokens, HEAD_SIZE), jnp.bfloat16),
            pltpu.VMEM((heads, 1, tokens), jnp.float32),
            pltpu.VMEM((heads, 1, tokens), jnp.float32),
            pltpu.VMEM((heads, HEAD_SIZE, tokens), jnp.float32),
            pltpu.SemaphoreType.DMA,
            pltpu.SemaphoreType.DMA((3, owners, KINDS)),
            pltpu.SemaphoreType.DMA((owners, KINDS)),
        ],
        compiler_params=pltpu.CompilerParams(
            collective_id=0, has_side_effects=True, vmem_limit_bytes=48 * 1024 * 1024
        ),
    )(queries, cos, sin, kv)
    pages_here = owners * rounds
    arranged = (
        raw.reshape(2, pages_here, PAGE_TOKENS, kv_local, HEAD_SIZE)
        .transpose(0, 3, 1, 2, 4)
        .reshape(2, kv_local, pages_here, PAGE_TOKENS * HEAD_SIZE)
    )
    source_index = jnp.arange(owners, dtype=jnp.int32)[:, None]
    round_index = jnp.arange(rounds, dtype=jnp.int32)[None, :]
    block_index = source_index * (tokens // PAGE_TOKENS) + round_index * owners + my_index
    target = block_table[block_index.reshape(-1)]
    paged = jnp.zeros_like(arranged).at[:, :, target].set(arranged)
    return (attended, paged[0], paged[1])


def solution(mesh):
    in_specs = (
        P(("groups", "seq"), "head"),
        P(("groups", "seq"), "head"),
        P(("groups", "seq"), "head"),
        P(("groups", "seq"), None, "head"),
        P(("groups", "seq"), None, "head"),
        P(None, ("groups", "seq")),
        P("groups"),
    )
    out_specs = (
        P(("groups", "seq"), "head"),
        P("head", ("groups", "seq"), None),
        P("head", ("groups", "seq"), None),
    )
    return jax.shard_map(shards, mesh=mesh, in_specs=in_specs, out_specs=out_specs, check_vma=False)
```

time: 330 us -> 116 us (0.35)
  matrix products: 112 us -> 0 us
  Pallas kernels: 0 us -> 103 us
  local copies, waits for them, and re-layouts: 88.5 us -> 10 us
  waiting for transfers between devices: 61.6 us -> 0 us
  other arithmetic: 43.5 us -> 2.03 us
  between operations: 14.1 us -> 0.83 us
  starting transfers between devices: 6.12 us -> 0 us
    dot_general x48 -> x0, matrix products: 112 us -> none  [the longest x24 60.7 us: update_block(): jnp.einsum('grk,gkd->grd', weights.astype(jnp.bfloat16), value_tile, pref...]
    pallas_call x0 -> x1, Pallas kernels: none -> 103 us  [shards(): pl.pallas_call(functools.partial(kernel, owners, kv_local, per_group), ou...]
    all_gather x4 -> x0, waiting for transfers between devices: 61.5 us -> none  [the longest x1 47.4 us: shards(): lax.all_gather(stored_values, 'seq', axis=0, tiled=True)]
    reduce_sum x24 -> x0, other arithmetic: 32.5 us -> none  [update_block(): denom = denom * factor + jnp.sum(weights, -1)]
    dynamic_slice x24 -> x0, local copies, waits for them, and re-layouts: 23.8 us -> none  [step_body(): lax.dynamic_slice_in_dim(values, offset, key_block, 0)]
    while x33 -> x0, local copies, waits for them, and re-layouts: 15.5 us -> none
    transpose x3 -> x1, local copies, waits for them, and re-layouts: 9.54 us -> 0.05 us  [shards(): arranged = raw.reshape(2, pages_here, PAGE_TOKENS, kv_local, HEAD_SIZE).t...]
    convert_element_type x2 -> x0, local copies, waits for them, and re-layouts: 9.05 us -> none  [shards(): attended = finished.reshape(kv_local, tok_rows, per_group, HEAD_SIZE).tra...]
  transfers between devices with their start and end apart: 5 -> 0, of which waited for: 2 -> 0; matrix products, arithmetic and copies ran while one was open for 51% -> 0% of each run, Pallas kernels for 0% -> 0%
where the time goes in v1:
time: 116 us
  Pallas kernels  103 us (89%)
  local copies, waits for them, and re-layouts  10 us (9%)
  other arithmetic  2.03 us (2%)
    pallas_call x1, Pallas kernels, shards(): pl.pallas_call(functools.partial(kernel, owners, kv_local, per_group), ou...  103 us
    unnamed x15, local copies, waits for them, and re-layouts  5.89 us

profile of v1, /device:TPU:28, one launch (start us, length us, event | category | flops | bytes accessed | tf_op | source)
XLA Modules:
  0.0 116.1 jit_solution(16094758768843685559)
XLA Ops:
  0.6 0.8 broadcast_in_dim.4
  1.4 0.1 reshape.109
  1.5 1.4 %fusion = (f32[3,256,64]{2,1,0:T(8,128)S(1)}, f32[3,256,64]{2,1,0:T(8,128)S(1)}, f32[3,256,64]{2,1,0:T(8,128)S(1)}) fusion(f32[64]{0:T(128)S(1)} %multiply_power_fusion, f32[3,256]{1,0:T(4,128)S(1)} %add_convert_fusion), kind=kLoop, calls=%fused_computation.16 | loop fusion | flops 98304 | bytes 593152 | tf_op jit(solution)/shard_map/neg | solution.py:201
  3.0 0.3 pad_maximum_fusion.1
  3.3 0.7 copy-done.2
  3.9 0.4 fusion.4
  4.4 0.9 copy-done.3
  5.3 0.4 fusion.3
  5.8 0.8 copy-done.4
  6.6 0.1 copy-done.5
  6.7 0.1 pad_maximum_fusion.kv_hbm
  6.8 1.1 copy-done.1
  7.9 103.2 %shard_map.94 = (bf16[256,1792]{1,0:T(8,128)(2,1)S(1)}, bf16[2,16,16,256]{3,2,1,0:T(8,128)(2,1)S(1)}) custom-call(bf16[256,1792]{1,0:T(8,128)(2,1)S(1)} %copy-done.1, f32[3,256,128]{2,1,0:T(8,128)S(1)} %get-tuple-element.25.cos_ref, f32[3,256,128]{2,1,0:T(8,128)S(1)} %get-tuple-element.26.sin_ref, bf16[3,2,256,256]{3,2,1,0:T(8,128)(2,1)S(1)} %pad_maximum_fusion.kv_hbm), custom_call_target="tpu_custom_call" | custom-call | tf_op jit(solution)/shard_map/pallas_call | solution.py:211
  111.1 0.1 reshape.110
  111.3 0.1 reshape.121
  111.4 0.1 add_add_fusion
  111.5 0.1 add.85
  111.6 0.7 gather_fusion
  112.2 0.1 broadcast_in_dim.5
  112.4 1.2 %scatter_fusion = bf16[2,2,16,2048]{3,1,2,0:T(2,128)(2,1)S(1)} fusion(bf16[2,2,16,2048]{3,1,2,0:T(2,128)(2,1)S(1)} %broadcast_in_dim.5, s32[16]{0:T(128)S(1)} %fusion.2, bf16[16,2,2,2048]{3,2,1,0:T(2,128)(2,1)S(1)} %bitcast.35), kind=kCustom, calls=%fused_computation.1 | custom fusion | bytes 786496 | tf_op jit(solution)/shard_map/scatter | solution.py:243
  113.6 0.2 slice_bitcast_fusion
  113.8 0.7 copy.22
  114.5 0.7 copy.23
  115.2 0.9 copy.34
  (23 shorter events, 0.3 us)
Async XLA Ops:
  0.6 110.9 %copy-start = (s32[128]{0:T(128)S(1)}, s32[128]{0:T(128)}, u32[]{:S(2)}) copy-start(s32[128]{0:T(128)} %param.13) | copy-start | bytes 1540
  3.0 1.0 copy-start.2
  4.3 1.0 copy-start.3
  5.7 0.9 copy-start.4
  5.7 1.0 copy-start.5
  6.7 1.2 %copy-start.1 = (bf16[256,1792]{1,0:T(8,128)(2,1)S(1)}, bf16[256,1792]{1,0:T(8,128)(2,1)}, u32[]{:S(2)}) copy-start(bf16[256,1792]{1,0:T(8,128)(2,1)} %q_ref.1) | copy-start | bytes 2752516

commit v2 on v1

--- a/solution.py
+++ b/solution.py
@@ -86,7 +86,7 @@
         for h in range(heads):
             x = q_ref[:, h * HEAD_SIZE : (h + 1) * HEAD_SIZE].astype(jnp.float32)
             y = x * cos + pltpu.roll(x, HEAD_SIZE // 2, 1) * sin
-            turned[part, h] = y.astype(jnp.bfloat16)
+            turned[part, h] = y.T.astype(jnp.bfloat16)
         return carry
 
     lax.fori_loop(0, KINDS, turn, 0)
@@ -95,29 +95,41 @@
     total[...] = jnp.zeros(total.shape, jnp.float32)
 
     def absorb(j, part, causal):
-        for g in range(kv_local):
-            columns = slice(g * HEAD_SIZE, (g + 1) * HEAD_SIZE)
-            keys = held[j, part, 0, :, columns]
-            values = held[j, part, 1, :, columns].T
-            for r in range(per_group):
-                h = g * per_group + r
-                scores = lax.dot_general(
-                    keys, turned[part, h], (((1,), (1,)), ((), ())),
-                    preferred_element_type=jnp.float32,
-                )
-                if causal:
-                    key_index = lax.broadcasted_iota(jnp.int32, scores.shape, 0)
-                    row_index = lax.broadcasted_iota(jnp.int32, scores.shape, 1)
-                    scores = jnp.where(key_index <= row_index, scores, masked_value)
-                old = top[h]
-                new = jnp.maximum(old, jnp.max(scores, 0, keepdims=True))
-                factor = jnp.exp2((old - new) * scale)
-                weights = jnp.exp2((scores - new) * scale)
-                top[h] = new
-                denom[h] = denom[h] * factor + jnp.sum(weights, 0, keepdims=True)
-                total[h] = total[h] * factor + jnp.dot(
-                    values, weights.astype(jnp.bfloat16), preferred_element_type=jnp.float32
-                )
+        keys = [held[j, part, 0, :, g * HEAD_SIZE : (g + 1) * HEAD_SIZE] for g in range(kv_local)]
+        values = [
+            held[j, part, 1, :, g * HEAD_SIZE : (g + 1) * HEAD_SIZE].T for g in range(kv_local)
+        ]
+
+        def score(h):
+            return jnp.dot(
+                keys[h // per_group], turned[part, h], preferred_element_type=jnp.float32
+            )
+
+        def add(h, weights, factor):
+            total[h] = total[h] * factor + jnp.dot(
+                values[h // per_group], weights, preferred_element_type=jnp.float32
+            )
+
+        pending = None
+        following = score(0)
+        for h in range(heads):
+            scores = following
+            if h + 1 < heads:
+                following = score(h + 1)
+            if causal:
+                key_index = lax.broadcasted_iota(jnp.int32, scores.shape, 0)
+                row_index = lax.broadcasted_iota(jnp.int32, scores.shape, 1)
+                scores = jnp.where(key_index <= row_index, scores, masked_value)
+            old = top[h]
+            new = jnp.maximum(old, jnp.max(scores, 0, keepdims=True))
+            factor = jnp.exp2((old - new) * scale)
+            weights = jnp.exp2((scores - new) * scale)
+            top[h] = new
+            denom[h] = denom[h] * factor + jnp.sum(weights, 0, keepdims=True)
+            if pending is not None:
+                add(*pending)
+            pending = (h, weights.astype(jnp.bfloat16), factor)
+        add(*pending)
 
     def own_step(part, carry):
         absorb(me, part, False)
@@ -218,7 +230,7 @@
         out_specs=(vmem, vmem),
         scratch_shapes=[
             pltpu.VMEM((owners, KINDS, 2, tokens, key_width), jnp.bfloat16),
-            pltpu.VMEM((KINDS, heads, tokens, HEAD_SIZE), jnp.bfloat16),
+            pltpu.VMEM((KINDS, heads, HEAD_SIZE, tokens), jnp.bfloat16),
             pltpu.VMEM((heads, 1, tokens), jnp.float32),
             pltpu.VMEM((heads, 1, tokens), jnp.float32),
             pltpu.VMEM((heads, HEAD_SIZE, tokens), jnp.float32),

time: 116 us -> 87 us (0.75)
  Pallas kernels: 103 us -> 73.8 us
    pallas_call x1, Pallas kernels: 103 us -> 73.8 us  [shards(): pl.pallas_call(functools.partial(kernel, owners, kv_local, per_group), ou...]
where the time goes in v2:
time: 87 us; the launch traced here: 86.7 us
  Pallas kernels  73.8 us (85%)
  local copies, waits for them, and re-layouts  10 us (11%)
  other arithmetic  2.03 us (2%)
    pallas_call x1, Pallas kernels, shards(): pl.pallas_call(functools.partial(kernel, owners, kv_local, per_group), ou...  73.8 us
    unnamed x15, local copies, waits for them, and re-layouts  5.89 us

profile of v2, /device:TPU:28, one launch (start us, length us, event | category | flops | bytes accessed | tf_op | source)
XLA Modules:
  0.0 86.7 jit_solution(17288627244757912659)
XLA Ops:
  0.6 0.8 broadcast_in_dim.4
  1.4 0.1 reshape.109
  1.5 1.4 %fusion = (f32[3,256,64]{2,1,0:T(8,128)S(1)}, f32[3,256,64]{2,1,0:T(8,128)S(1)}, f32[3,256,64]{2,1,0:T(8,128)S(1)}) fusion(f32[64]{0:T(128)S(1)} %multiply_power_fusion, f32[3,256]{1,0:T(4,128)S(1)} %add_convert_fusion), kind=kLoop, calls=%fused_computation.16 | loop fusion | flops 98304 | bytes 593152 | tf_op jit(solution)/shard_map/neg | solution.py:213
  3.0 0.3 pad_maximum_fusion.1
  3.3 0.7 copy-done.2
  3.9 0.4 fusion.4
  4.4 0.9 %copy-done.3 = bf16[256,2,256]{2,1,0:T(2,128)(2,1)S(1)} copy-done((bf16[256,2,256]{2,1,0:T(2,128)(2,1)S(1)}, bf16[256,2,256]{2,1,0:T(2,128)(2,1)}, u32[]{:S(2)}) %copy-start.3) | copy-done | bytes 262168
  5.3 0.4 fusion.3
  5.8 0.8 copy-done.4
  6.6 0.1 copy-done.5
  6.7 0.1 pad_maximum_fusion.kv_hbm
  6.8 1.1 %copy-done.1 = bf16[256,1792]{1,0:T(8,128)(2,1)S(1)} copy-done((bf16[256,1792]{1,0:T(8,128)(2,1)S(1)}, bf16[256,1792]{1,0:T(8,128)(2,1)}, u32[]{:S(2)}) %copy-start.1) | copy-done | bytes 917528
  7.9 73.8 %shard_map.94 = (bf16[256,1792]{1,0:T(8,128)(2,1)S(1)}, bf16[2,16,16,256]{3,2,1,0:T(8,128)(2,1)S(1)}) custom-call(bf16[256,1792]{1,0:T(8,128)(2,1)S(1)} %copy-done.1, f32[3,256,128]{2,1,0:T(8,128)S(1)} %get-tuple-element.25.cos_ref, f32[3,256,128]{2,1,0:T(8,128)S(1)} %get-tuple-element.26.sin_ref, bf16[3,2,256,256]{3,2,1,0:T(8,128)(2,1)S(1)} %pad_maximum_fusion.kv_hbm), custom_call_target="tpu_custom_call" | custom-call | tf_op jit(solution)/shard_map/pallas_call | solution.py:223
  81.7 0.1 reshape.110
  81.9 0.1 reshape.121
  82.0 0.1 add_add_fusion
  82.0 0.1 add.85
  82.1 0.7 gather_fusion
  82.8 0.1 broadcast_in_dim.5
  83.0 1.2 %scatter_fusion = bf16[2,2,16,2048]{3,1,2,0:T(2,128)(2,1)S(1)} fusion(bf16[2,2,16,2048]{3,1,2,0:T(2,128)(2,1)S(1)} %broadcast_in_dim.5, s32[16]{0:T(128)S(1)} %fusion.2, bf16[16,2,2,2048]{3,2,1,0:T(2,128)(2,1)S(1)} %bitcast.35), kind=kCustom, calls=%fused_computation.1 | custom fusion | bytes 786496 | tf_op jit(solution)/shard_map/scatter | solution.py:255
  84.2 0.2 slice_bitcast_fusion
  84.4 0.7 copy.22
  85.1 0.7 copy.23
  85.8 0.9 %copy.34 = bf16[256,1792]{1,0:T(8,128)(2,1)} copy(bf16[256,1792]{1,0:T(8,128)(2,1)S(1)} %get-tuple-element.34) | data formatting | bytes 1835008
  (23 shorter events, 0.3 us)
Async XLA Ops:
  0.6 81.5 %copy-start = (s32[128]{0:T(128)S(1)}, s32[128]{0:T(128)}, u32[]{:S(2)}) copy-start(s32[128]{0:T(128)} %param.13) | copy-start | bytes 1540
  3.0 1.0 %copy-start.2 = (bf16[256,2,256]{2,1,0:T(2,128)(2,1)S(1)}, bf16[256,2,256]{2,1,0:T(2,128)(2,1)}, u32[]{:S(2)}) copy-start(bf16[256,2,256]{2,1,0:T(2,128)(2,1)} %param.11) | copy-start | bytes 786436
  4.3 1.0 %copy-start.3 = (bf16[256,2,256]{2,1,0:T(2,128)(2,1)S(1)}, bf16[256,2,256]{2,1,0:T(2,128)(2,1)}, u32[]{:S(2)}) copy-start(bf16[256,2,256]{2,1,0:T(2,128)(2,1)} %param.10) | copy-start | bytes 786436
  5.7 0.9 %copy-start.4 = (bf16[256,256]{1,0:T(8,128)(2,1)S(1)}, bf16[256,256]{1,0:T(8,128)(2,1)}, u32[]{:S(2)}) copy-start(bf16[256,256]{1,0:T(8,128)(2,1)} %param.9) | copy-start | bytes 393220
  5.7 1.0 %copy-start.5 = (bf16[256,256]{1,0:T(8,128)(2,1)S(1)}, bf16[256,256]{1,0:T(8,128)(2,1)}, u32[]{:S(2)}) copy-start(bf16[256,256]{1,0:T(8,128)(2,1)} %param.8) | copy-start | bytes 393220
  6.7 1.2 %copy-start.1 = (bf16[256,1792]{1,0:T(8,128)(2,1)S(1)}, bf16[256,1792]{1,0:T(8,128)(2,1)}, u32[]{:S(2)}) copy-start(bf16[256,1792]{1,0:T(8,128)(2,1)} %q_ref.1) | copy-start | bytes 2752516

commit v3 on v2

--- a/solution.py
+++ b/solution.py
@@ -22,19 +22,25 @@
 
 
 def kernel(
-    n, kv_local, per_group, q_ref, cos_ref, sin_ref, kv_hbm, out_ref, raw_ref,
-    held, turned, top, denom, total, own_sem, send_sem, recv_sem,
+    n, kv_local, per_group, q_hbm, cos_ref, sin_ref, stored_ref, keys_hbm, values_hbm,
+    out_ref, raw_ref, q_ref, held, turned, top, denom, total, own_sem, send_sem, recv_sem,
 ):
     me = lax.axis_index("seq")
     partner = me + 1 - 2 * (me % 2)
-    tokens = q_ref.shape[0]
+    tokens = q_hbm.shape[0]
     heads = kv_local * per_group
     scale = HEAD_SIZE ** -0.5 * math.log2(math.e)
     has_right = me + 2 < n
     has_left = me - 2 >= 0
 
-    own = pltpu.make_async_copy(kv_hbm, held.at[me], own_sem)
-    own.start()
+    own = [
+        pltpu.make_async_copy(stored_ref, held.at[me, pl.ds(0, PRIOR_SEGMENTS)], own_sem.at[0]),
+        pltpu.make_async_copy(keys_hbm, held.at[me, OWN_PART, 0], own_sem.at[1]),
+        pltpu.make_async_copy(values_hbm, held.at[me, OWN_PART, 1], own_sem.at[2]),
+        pltpu.make_async_copy(q_hbm, q_ref, own_sem.at[3]),
+    ]
+    for copy in own:
+        copy.start()
     barrier = pltpu.get_barrier_semaphore()
     pl.semaphore_signal(barrier, inc=1, device_id={"seq": partner}, device_id_type=MESH)
 
@@ -48,7 +54,8 @@
 
     expected = 1 + has_right.astype(jnp.int32) + has_left.astype(jnp.int32)
     pl.semaphore_wait(barrier, expected)
-    own.wait()
+    for copy in own[:3]:
+        copy.wait()
 
     def remote(way, j, part):
         target = (me + 2, me - 2, partner)[way]
@@ -65,10 +72,12 @@
         mine = (j % 2) == (me % 2)
         stored = part < PRIOR_SEGMENTS
         if way == RIGHT:
-            return mine & (j <= me) & has_right
+            relayed = (j == partner) & (part == 0) & (me + 4 >= n)
+            return ((mine & (j <= me)) | relayed) & has_right
         if way == LEFT:
             return mine & (j >= me) & stored & has_left
-        return mine & (stored | (j <= partner))
+        relayed = (j == me - 2) & (part == 0) & (me + 2 >= n)
+        return mine & (stored | (j <= partner)) & jnp.logical_not(relayed)
 
     def forward(j, part):
         for way in (ACROSS, RIGHT, LEFT):
@@ -79,6 +88,7 @@
 
     for part in range(KINDS):
         forward(me, part)
+    own[3].wait()
 
     def turn(part, carry):
         cos = cos_ref[part]
@@ -211,14 +221,14 @@
     sin = jnp.sin(angles)
     cos = jnp.concatenate([cos, cos], -1)
     sin = jnp.concatenate([-sin, sin], -1)
-    kv = jnp.stack(
+    stored = jnp.stack(
         [
             jnp.stack([stored_keys[:, s, :], stored_values[:, s, :]])
             for s in range(PRIOR_SEGMENTS)
         ]
-        + [jnp.stack([current_keys, current_values])]
     )
     rounds = tokens // PAGE_TOKENS // owners
+    hbm = pl.BlockSpec(memory_space=pltpu.HBM)
     vmem = pl.BlockSpec(memory_space=pltpu.VMEM)
     attended, raw = pl.pallas_call(
         functools.partial(kernel, owners, kv_local, per_group),
@@ -226,22 +236,23 @@
             jax.ShapeDtypeStruct((tokens, width), jnp.bfloat16),
             jax.ShapeDtypeStruct((2, owners * rounds, PAGE_TOKENS, key_width), jnp.bfloat16),
         ),
-        in_specs=[vmem, vmem, vmem, pl.BlockSpec(memory_space=pl.ANY)],
+        in_specs=[hbm, vmem, vmem, vmem, hbm, hbm],
         out_specs=(vmem, vmem),
         scratch_shapes=[
+            pltpu.VMEM((tokens, width), jnp.bfloat16),
             pltpu.VMEM((owners, KINDS, 2, tokens, key_width), jnp.bfloat16),
             pltpu.VMEM((KINDS, heads, HEAD_SIZE, tokens), jnp.bfloat16),
             pltpu.VMEM((heads, 1, tokens), jnp.float32),
             pltpu.VMEM((heads, 1, tokens), jnp.float32),
             pltpu.VMEM((heads, HEAD_SIZE, tokens), jnp.float32),
-            pltpu.SemaphoreType.DMA,
+            pltpu.SemaphoreType.DMA((4,)),
             pltpu.SemaphoreType.DMA((3, owners, KINDS)),
             pltpu.SemaphoreType.DMA((owners, KINDS)),
         ],
         compiler_params=pltpu.CompilerParams(
             collective_id=0, has_side_effects=True, vmem_limit_bytes=48 * 1024 * 1024
         ),
-    )(queries, cos, sin, kv)
+    )(queries, cos, sin, stored, current_keys, current_values)
     pages_here = owners * rounds
     arranged = (
         raw.reshape(2, pages_here, PAGE_TOKENS, kv_local, HEAD_SIZE)

time: 87 us -> 83.8 us (0.963)
  Pallas kernels: 73.8 us -> 71.6 us
    pallas_call x1, Pallas kernels: 73.8 us -> 71.6 us  [shards(): pl.pallas_call(functools.partial(kernel, owners, kv_local, per_group), ou...]
    unnamed x15, local copies, waits for them, and re-layouts: 5.89 us -> 5 us
where the time goes in v3:
time: 83.8 us; the launch traced here: 83.6 us
  Pallas kernels  71.6 us (85%)
  local copies, waits for them, and re-layouts  9.14 us (11%)
  other arithmetic  1.96 us (2%)
    pallas_call x1, Pallas kernels, shards(): pl.pallas_call(functools.partial(kernel, owners, kv_local, per_group), ou...  71.6 us
    unnamed x15, local copies, waits for them, and re-layouts  5 us

profile of v3, /device:TPU:28, one launch (start us, length us, event | category | flops | bytes accessed | tf_op | source)
XLA Modules:
  0.0 83.6 jit_solution(13449705539443444670)
XLA Ops:
  0.6 0.0 copy-start
  0.6 0.8 broadcast_in_dim.4
  1.4 0.1 reshape.109
  1.5 1.4 %fusion = (f32[3,256,64]{2,1,0:T(8,128)S(1)}, f32[3,256,64]{2,1,0:T(8,128)S(1)}, f32[3,256,64]{2,1,0:T(8,128)S(1)}) fusion(f32[64]{0:T(128)S(1)} %multiply_power_fusion, f32[3,256]{1,0:T(4,128)S(1)} %add_convert_fusion), kind=kLoop, calls=%fused_computation.15 | loop fusion | flops 98304 | bytes 593152 | tf_op jit(solution)/shard_map/neg | solution.py:223
  3.0 0.3 pad_maximum_fusion.1
  3.3 0.7 copy-done.4
  3.9 0.4 fusion.4
  4.4 0.9 %copy-done.5 = bf16[256,2,256]{2,1,0:T(2,128)(2,1)S(1)} copy-done((bf16[256,2,256]{2,1,0:T(2,128)(2,1)S(1)}, bf16[256,2,256]{2,1,0:T(2,128)(2,1)}, u32[]{:S(2)}) %copy-start.5) | copy-done | bytes 262168
  5.3 0.4 fusion.3
  5.8 0.1 pad_maximum_fusion.stored_ref
  5.8 1.1 %copy-done.1 = bf16[256,1792]{1,0:T(8,128)(2,1)S(1)} copy-done((bf16[256,1792]{1,0:T(8,128)(2,1)S(1)}, bf16[256,1792]{1,0:T(8,128)(2,1)}, u32[]{:S(2)}) %copy-start.1) | copy-done | bytes 917528
  6.9 0.0 copy-done.3
  6.9 71.6 %shard_map.94 = (bf16[256,1792]{1,0:T(8,128)(2,1)S(1)}, bf16[2,16,16,256]{3,2,1,0:T(8,128)(2,1)S(1)}) custom-call(bf16[256,1792]{1,0:T(8,128)(2,1)S(1)} %copy-done.1, f32[3,256,128]{2,1,0:T(8,128)S(1)} %get-tuple-element.25.cos_ref, f32[3,256,128]{2,1,0:T(8,128)S(1)} %get-tuple-element.26.sin_ref, bf16[2,2,256,256]{3,2,1,0:T(8,128)(2,1)S(1)} %pad_maximum_fusion.stored_ref, ...), custom_call_target="tpu_custom_call" | custom-call | tf_op jit(solution)/shard_map/pallas_call | solution.py:233
  78.6 0.1 reshape.110
  78.7 0.1 reshape.121
  78.8 0.1 add_add_fusion
  78.9 0.1 add.85
  79.0 0.7 gather_fusion
  79.7 0.1 broadcast_in_dim.5
  79.8 1.2 %scatter_fusion = bf16[2,2,16,2048]{3,1,2,0:T(2,128)(2,1)S(1)} fusion(bf16[2,2,16,2048]{3,1,2,0:T(2,128)(2,1)S(1)} %broadcast_in_dim.5, s32[16]{0:T(128)S(1)} %fusion.2, bf16[16,2,2,2048]{3,2,1,0:T(2,128)(2,1)S(1)} %bitcast.31), kind=kCustom, calls=%fused_computation.1 | custom fusion | bytes 786496 | tf_op jit(solution)/shard_map/scatter | solution.py:266
  81.1 0.2 slice_bitcast_fusion
  81.2 0.7 copy.22
  81.9 0.7 copy.23
  82.6 0.9 %copy.34 = bf16[256,1792]{1,0:T(8,128)(2,1)} copy(bf16[256,1792]{1,0:T(8,128)(2,1)S(1)} %get-tuple-element.34) | data formatting | bytes 1835008
  (22 shorter events, 0.3 us)
Async XLA Ops:
  0.6 78.4 %copy-start = (s32[128]{0:T(128)S(1)}, s32[128]{0:T(128)}, u32[]{:S(2)}) copy-start(s32[128]{0:T(128)} %param.13) | copy-start | bytes 1540
  3.0 1.0 %copy-start.4 = (bf16[256,2,256]{2,1,0:T(2,128)(2,1)S(1)}, bf16[256,2,256]{2,1,0:T(2,128)(2,1)}, u32[]{:S(2)}) copy-start(bf16[256,2,256]{2,1,0:T(2,128)(2,1)} %param.11) | copy-start | bytes 786436
  4.3 1.0 %copy-start.5 = (bf16[256,2,256]{2,1,0:T(2,128)(2,1)S(1)}, bf16[256,2,256]{2,1,0:T(2,128)(2,1)}, u32[]{:S(2)}) copy-start(bf16[256,2,256]{2,1,0:T(2,128)(2,1)} %param.10) | copy-start | bytes 786436
  5.7 1.2 %copy-start.1 = (bf16[256,1792]{1,0:T(8,128)(2,1)S(1)}, bf16[256,1792]{1,0:T(8,128)(2,1)}, u32[]{:S(2)}) copy-start(bf16[256,1792]{1,0:T(8,128)(2,1)} %q_hbm.1) | copy-start | bytes 2752516
  5.8 1.1 %copy-start.2 = (bf16[256,256]{1,0:T(8,128)(2,1)S(1)}, bf16[256,256]{1,0:T(8,128)(2,1)}, u32[]{:S(2)}) copy-start(bf16[256,256]{1,0:T(8,128)(2,1)} %keys_hbm.1) | copy-start | bytes 393220
  5.8 1.2 %copy-start.3 = (bf16[256,256]{1,0:T(8,128)(2,1)S(1)}, bf16[256,256]{1,0:T(8,128)(2,1)}, u32[]{:S(2)}) copy-start(bf16[256,256]{1,0:T(8,128)(2,1)} %values_hbm.1) | copy-start | bytes 393220
